TPU v7x, 256 devices: a whole 4x4x8 slice. The times are simulated.
256 devices in a mesh: layer: 4 (over y), row: 8 (over x, z_lo), col: 8 (over z_hi, core).
Axes of the slice: x: 4, y: 4, z: 8 (z_hi: 4, z_lo: 2; z = z_hi * 2 + z_lo), core: 2. Of those that a mesh axis runs over, the one named last changes fastest.
Arguments:
- ancestor: float32 [8192, 8192], P('row', 'col'), may hold values from -768 to 3840, as said below
- coupling: bfloat16 [4, 8192, 1024], P('layer', ('row', 'col')), may hold values from -10 to 10
- fronts: float32 [4, 2, 512, 512], P('layer', None, None, ('row', 'col')), may hold values from -10 to 360, as said below
- tile_pattern: int32 [4, 2, 8], P('layer'), may hold values 0 or 1
Outputs:
- schur: float32 [8192, 8192], P('row', 'col')
- panel_factor: float32 [8192, 512], P(('row', 'col'))
- pivots: float32 [512], P(('row', 'col'))
Inputs may be any that keep to these rules, and one draw needn't show every extreme that they name: `ancestor`: symmetric and positive definite; the leading [512, 512] block of schur_0 stays positive definite after all layers' terms are subtracted. `fronts`: each [512, 512] block is symmetric and positive definite, with diagonal entries from 200 to 360 and other entries within -10 to 10.
All inputs are finite; a program needn't handle non-finite values. No bound on the sum of `tile_pattern` on one device may be relied on, other than what follows from the above.
Results may differ from a plain program's by a relative error of at most 0.0008.
Values may be sent and summed in bfloat16 or wider, within the bound.
A program may use at most 128 MiB of HBM per device.

v0:
```python
import jax
import jax.numpy as jnp
from jax import lax
from jax.sharding import PartitionSpec as P

S = 8192
TILE = 1024
P_SIZE = 512
NP = 2


def spread(value, axis, source):
    kept = jnp.where(lax.axis_index(axis) == source, value, 0).astype(value.dtype)
    return lax.psum(kept, axis)


def filled_up(lines, size):
    spare = -len(lines) % size
    return jnp.pad(lines, [(0, spare)] + [(0, 0)] * (lines.ndim - 1))


def spread_2(x, axis, root):
    lines = jnp.where(lax.axis_index(axis) == root, x, jnp.zeros_like(x)).reshape(
        -1, *x.shape[1:][-1:]
    )
    padded = filled_up(lines, lax.axis_size(axis))
    own = lax.psum_scatter(padded, axis, scatter_dimension=0, tiled=True)
    return lax.all_gather(own, axis, axis=0, tiled=True)[: len(lines)].reshape(x.shape)


def column_block(sender):
    row_count = lax.axis_size("row")
    col_count = lax.axis_size("col")
    col_place = lax.axis_index("col")
    first_root = col_place * row_count // col_count
    pieces = sender(first_root + 0)
    return pieces


def solve_rows(factor, columns):
    return lax.linalg.triangular_solve(
        factor, columns, left_side=False, lower=True, transpose_a=True
    )


def local(ancestor, coupling, fronts, tile_pattern):
    row_count = lax.axis_size("row")
    col_count = lax.axis_size("col")
    row_place = lax.axis_index("row")
    col_place = lax.axis_index("col")
    local_rows = S // (row_count * col_count)
    block_rows = S // row_count
    gathered = lax.all_gather(
        fronts.astype(jnp.bfloat16), ("row", "col"), axis=3, tiled=True
    ).astype(fronts.dtype)
    factors = jnp.linalg.cholesky(gathered[0])
    first_row = (row_place * col_count + col_place) * local_rows
    positions = first_row + lax.iota(jnp.int32, local_rows)
    onehot = (positions[:, None] // TILE == lax.iota(jnp.int32, S // TILE)[None, :]).astype(
        jnp.float32
    )
    row_masks = jnp.dot(onehot, tile_pattern[0].T.astype(jnp.float32))
    solved_parts = []
    for panel in range(NP):
        columns = (
            coupling[0, :, panel * P_SIZE : (panel + 1) * P_SIZE].astype(jnp.float32)
            * row_masks[:, panel : panel + 1]
        )
        solved_parts.append(solve_rows(factors[panel], columns))
    scaled = jnp.concatenate(solved_parts, 1).astype(jnp.bfloat16)
    row_side = lax.all_gather(scaled, "col", axis=0, tiled=True)
    col_side = column_block(lambda source: spread(row_side, "row", source))
    update = -lax.dot_general(
        row_side, col_side, (((1,), (1,)), ((), ())), preferred_element_type=jnp.float32
    )
    shared = lax.psum_scatter(
        update.astype(jnp.bfloat16), "layer", scatter_dimension=0, tiled=True
    ).astype(jnp.float32)
    summed = lax.all_gather(shared.astype(jnp.bfloat16), "layer", axis=0, tiled=True).astype(
        shared.dtype
    )
    leading = ancestor[:, :P_SIZE] + summed[:, :P_SIZE]
    global_rows = row_place * block_rows + lax.iota(jnp.int32, block_rows)
    trailing = None
    working = leading
    pivot_source = working[0:P_SIZE, 0:P_SIZE]
    pivot_block = spread(pivot_source, ("row", "col"), 0)
    pivot_chol = jnp.linalg.cholesky(pivot_block)
    keep_rows = (global_rows >= 0)[:, None]
    received = spread_2(working, "col", 0)
    solved = solve_rows(pivot_chol, received)
    panel_rows = jnp.where(keep_rows, solved, jnp.zeros_like(solved))
    panel_cols = column_block(lambda source: spread(panel_rows, "row", source))
    leading = leading - jnp.dot(
        panel_rows,
        panel_cols[:P_SIZE].T,
        precision=lax.Precision.HIGHEST,
        preferred_element_type=jnp.float32,
    )
    history = (panel_rows, panel_cols)
    panel_outs = lax.dynamic_slice_in_dim(panel_rows, col_place * local_rows, local_rows, 0)
    diagonal = jnp.diagonal(pivot_chol)
    pivot_outs = diagonal * diagonal
    trailing = ancestor[:, P_SIZE:] + summed[:, P_SIZE:]
    rows_part, cols_part = history
    trailing = trailing - jnp.dot(
        rows_part,
        cols_part[P_SIZE:].T,
        precision=lax.Precision.HIGHEST,
        preferred_element_type=jnp.float32,
    )
    schur = jnp.concatenate([leading, trailing], 1)
    pivot_share = pivot_outs.shape[0] // (row_count * col_count)
    flat_place = row_place * col_count + col_place
    my_pivots = lax.dynamic_slice_in_dim(pivot_outs, flat_place * pivot_share, pivot_share, 0)
    return (schur, panel_outs, my_pivots)


def solution(mesh):
    return jax.shard_map(
        local,
        mesh=mesh,
        in_specs=(
            P("row", "col"),
            P("layer", ("row", "col"), None),
            P("layer", None, None, ("row", "col")),
            P("layer", None, None),
        ),
        out_specs=(P("row", "col"), P(("row", "col"), None), P(("row", "col"))),
        check_vma=False,
    )
```

profile of v0, /device:TPU:1, one launch (start us, length us, event | category | flops | bytes accessed | tf_op | source)
XLA Modules:
  0.0 1092.8 jit_solution(2963737448343294521)
XLA Ops:
  7.2 1.4 convert_element_type.39
  10.1 1.9 convert_multiply_fusion.1
  12.0 115.7 %all-gather.5.cloned.1.call-done = bf16[1,2,512,512]{2,3,1,0:T(8,128)(2,1)} async-done(((bf16[1,2,512,8]{2,3,1,0:T(8,128)(2,1)}), bf16[1,2,512,512]{2,3,1,0:T(8,128)(2,1)}) %all-gather.5.cloned.1.call-update) | async-done | bytes 1048592 | tf_op jit(solution)/shard_map/all_gather | solution.py:53
  127.7 2.8 bitcast_convert_fusion
  130.6 2.0 copy.53
  132.9 1.3 copy-done.4
  134.3 23.5 %custom-call.64 = f32[2,128,128]{2,1,0:T(8,128)S(1)} custom-call(f32[2,128,128]{2,1,0:T(8,128)S(1)} %cholesky.531), custom_call_target="Cholesky" | custom-call | tf_op jit(solution)/shard_map/jit(cholesky)/cholesky | solution.py:56
  157.8 19.7 %custom-call.65 = f32[2,1,128,128]{2,3,1,0:T(8,128)S(1)} custom-call(f32[2,1,128,128]{3,2,1,0:T(8,128)S(1)} %select_bitcast_fusion.2), custom_call_target="InvertDiagBlocksLowerTriangular" | custom-call | tf_op jit(solution)/shard_map/jit(cholesky)/cholesky | solution.py:56
  177.7 1.5 constant_dynamic-update-slice_fusion.4
  179.2 1.5 convolution_subtract_fusion.3
  180.7 23.5 %custom-call.66 = f32[2,128,128]{2,1,0:T(8,128)S(1)} custom-call(f32[2,128,128]{2,1,0:T(8,128)S(1)} %cholesky.535), custom_call_target="Cholesky" | custom-call | tf_op jit(solution)/shard_map/jit(cholesky)/cholesky | solution.py:56
  204.2 20.1 %custom-call.67 = f32[2,1,128,128]{2,3,1,0:T(8,128)S(1)} custom-call(f32[2,1,128,128]{3,2,1,0:T(8,128)S(1)} %get-tuple-element.98), custom_call_target="InvertDiagBlocksLowerTriangular" | custom-call | tf_op jit(solution)/shard_map/jit(cholesky)/cholesky | solution.py:56
  224.8 1.6 convolution_subtract_fusion.4
  226.3 23.5 %custom-call.68 = f32[2,128,128]{2,1,0:T(8,128)S(1)} custom-call(f32[2,128,128]{2,1,0:T(8,128)S(1)} %cholesky.540), custom_call_target="Cholesky" | custom-call | tf_op jit(solution)/shard_map/jit(cholesky)/cholesky | solution.py:56
  249.8 19.7 %custom-call.69 = f32[2,1,128,128]{2,3,1,0:T(8,128)S(1)} custom-call(f32[2,1,128,128]{3,2,1,0:T(8,128)S(1)} %get-tuple-element.96), custom_call_target="InvertDiagBlocksLowerTriangular" | custom-call | tf_op jit(solution)/shard_map/jit(cholesky)/cholesky | solution.py:56
  269.8 1.5 convolution_subtract_fusion.7
  271.3 23.6 %custom-call.70 = f32[2,128,128]{2,1,0:T(8,128)S(1)} custom-call(f32[2,128,128]{2,1,0:T(8,128)S(1)} %convolution_subtract_fusion.7), custom_call_target="Cholesky" | custom-call | tf_op jit(solution)/shard_map/jit(cholesky)/cholesky | solution.py:56
  296.0 8.5 while.6
  296.7 1.4 bitcast_dynamic-update-slice_fusion.7
  298.8 1.4 bitcast_dynamic-update-slice_fusion.7
  300.9 1.4 bitcast_dynamic-update-slice_fusion.7
  303.1 1.4 bitcast_dynamic-update-slice_fusion.7
  304.5 39.3 %custom-call.78 = f32[4,128,128]{1,2,0:T(8,128)S(1)} custom-call(f32[4,128,128]{2,1,0:T(8,128)S(1)} %get-tuple-element.26), custom_call_target="InvertDiagBlocksLowerTriangular" | custom-call | tf_op jit(solution)/shard_map/triangular_solve/custom-call.14 | solution.py:41
  343.9 8.5 while.7
  344.5 1.4 bitcast_dynamic-update-slice_fusion.8
  346.7 1.4 bitcast_dynamic-update-slice_fusion.8
  348.8 1.4 bitcast_dynamic-update-slice_fusion.8
  350.9 1.4 bitcast_dynamic-update-slice_fusion.8
  352.3 39.5 %custom-call.79 = f32[4,128,128]{1,2,0:T(8,128)S(1)} custom-call(f32[4,128,128]{2,1,0:T(8,128)S(1)} %get-tuple-element.27), custom_call_target="InvertDiagBlocksLowerTriangular" | custom-call | tf_op jit(solution)/shard_map/triangular_solve/custom-call.14 | solution.py:41
  397.5 38.6 %all-gather.7.cloned.1.call-done = bf16[1024,1024]{0,1:T(8,128)(2,1)} async-done(((bf16[128,1024]{0,1:T(8,128)(2,1)}), bf16[1024,1024]{0,1:T(8,128)(2,1)}) %all-gather.7.cloned.1.call-update) | async-done | bytes 2097168 | tf_op jit(solution)/shard_map/all_gather | solution.py:71
  436.1 1.5 broadcast_select_fusion
  437.7 108.4 %all-reduce.6.cloned.1.call-done = bf16[1024,1024]{0,1:T(8,128)(2,1)} async-done(((bf16[1024,1024]{0,1:T(8,128)(2,1)}), bf16[1024,1024]{0,1:T(8,128)(2,1)}) %all-reduce.6.cloned.1.call-update) | async-done | bytes 2097168 | tf_op jit(solution)/shard_map/psum | solution.py:14
  546.1 5.3 negate_convert_fusion
  551.5 32.3 %reduce-scatter.3.cloned.1.call-done = bf16[256,1024]{0,1:T(8,128)(2,1)} async-done(((bf16[1024,1024]{0,1:T(8,128)(2,1)}), bf16[256,1024]{0,1:T(8,128)(2,1)}) %reduce-scatter.3.cloned.1.call-update) | async-done | bytes 524304 | tf_op jit(solution)/shard_map/reduce_scatter | solution.py:76
  583.8 4.7 fusion.95
  588.5 1.9 copy.86
  590.4 29.9 %all-gather.9.cloned.1.call-done = bf16[1024,1024]{0,1:T(8,128)(2,1)} async-done(((bf16[256,1024]{0,1:T(8,128)(2,1)}), bf16[1024,1024]{0,1:T(8,128)(2,1)}) %all-gather.9.cloned.1.call-update) | async-done | bytes 2097168 | tf_op jit(solution)/shard_map/all_gather | solution.py:79
  620.4 2.0 convert_element_type.47
  622.4 2.4 broadcast_select_fusion.2
  628.7 186.0 %all-reduce.8.cloned.1.call-done = f32[512,512]{0,1:T(8,128)} async-done(((f32[512,512]{0,1:T(8,128)}), f32[512,512]{0,1:T(8,128)}) %all-reduce.8.cloned.1.call-update) | async-done | bytes 1048592 | tf_op jit(solution)/shard_map/psum | solution.py:14
  814.7 1.6 copy.61
  816.6 11.7 %cholesky.467 = f32[128,128]{1,0:T(8,128)S(1)} custom-call(f32[128,128]{1,0:T(8,128)S(1)} %cholesky.544), custom_call_target="Cholesky" | custom-call | tf_op jit(solution)/shard_map/jit(cholesky)/cholesky | solution.py:88
  828.4 9.8 custom-call.71
  839.1 11.7 %cholesky.483 = f32[128,128]{1,0:T(8,128)S(1)} custom-call(f32[128,128]{1,0:T(8,128)S(1)} %cholesky.548), custom_call_target="Cholesky" | custom-call | tf_op jit(solution)/shard_map/jit(cholesky)/cholesky | solution.py:88
  850.9 9.9 custom-call.72
  862.1 11.7 %cholesky.504 = f32[128,128]{1,0:T(8,128)S(1)} custom-call(f32[128,128]{1,0:T(8,128)S(1)} %cholesky.553), custom_call_target="Cholesky" | custom-call | tf_op jit(solution)/shard_map/jit(cholesky)/cholesky | solution.py:88
  873.9 9.8 custom-call.73
  884.5 11.7 %cholesky.521 = f32[128,128]{1,0:T(8,128)S(1)} custom-call(f32[128,128]{1,0:T(8,128)S(1)} %convolution_subtract_fusion.12), custom_call_target="Cholesky" | custom-call | tf_op jit(solution)/shard_map/jit(cholesky)/cholesky | solution.py:88
  901.8 8.4 while.5
  902.6 1.3 dynamic-slice.20
  904.7 1.3 dynamic-slice.20
  906.7 1.3 dynamic-slice.20
  908.7 1.3 dynamic-slice.20
  910.2 39.3 %custom-call.74 = f32[4,128,128]{1,2,0:T(8,128)S(1)} custom-call(f32[4,128,128]{2,1,0:T(8,128)S(1)} %get-tuple-element.19), custom_call_target="InvertDiagBlocksLowerTriangular" | custom-call | tf_op jit(solution)/shard_map/triangular_solve | solution.py:41
  949.5 1.8 fusion.20
  951.3 1.7 convolution_subtract_fusion.2
  956.8 2.0 broadcast_select_fusion.1
  958.8 2.9 copy.87
  961.8 4.8 gather_fusion
  968.0 99.3 %all-reduce.10.cloned.1.call-done = f32[1024,512]{0,1:T(8,128)} async-done(((f32[1024,512]{0,1:T(8,128)}), f32[1024,512]{0,1:T(8,128)}) %all-reduce.10.cloned.1.call-update) | async-done | bytes 2097168 | tf_op jit(solution)/shard_map/psum | solution.py:14
  1067.3 5.7 convolution_subtract_fusion
  1073.0 5.0 fusion
  1078.0 2.5 pad_maximum_fusion
  1080.5 5.3 copy.74
  (159 shorter events, 33.1 us)
Async XLA Ops:
  7.2 120.6 %all-gather.5.cloned.1.call-start = ((), (), s32[]{:S(2)}) async-start(), calls=%async_computation.2 | async-start | bytes 1064960 | tf_op jit(solution)/shard_map/all_gather | solution.py:53
  8.6 427.5 %all-gather.7.cloned.1.call-start = ((), (), s32[]{:S(2)}) async-start(), calls=%async_computation.3 | async-start | bytes 2359296 | tf_op jit(solution)/shard_map/all_gather | solution.py:71
  130.6 2.0 copy-start.5
  132.9 1.3 copy-start.4
  295.9 95.9 %copy-start.10 = (f32[128,512]{1,0:T(8,128)S(1)}, f32[128,512]{1,0:T(8,128)}, u32[]{:S(2)}) copy-start(f32[128,512]{1,0:T(8,128)} %get-tuple-element.93) | copy-start | bytes 786436
  296.0 98.3 %copy-start.9 = (f32[128,512]{1,0:T(8,128)S(1)}, f32[128,512]{1,0:T(8,128)}, u32[]{:S(2)}) copy-start(f32[128,512]{1,0:T(8,128)} %get-tuple-element.94) | copy-start | bytes 786436
  397.4 148.6 %all-reduce.6.cloned.1.call-start = ((), (), s32[]{:S(2)}) async-start(), calls=%async_computation.4 | async-start | bytes 4194304 | tf_op jit(solution)/shard_map/psum | solution.py:14
  437.6 108.5 %copy-start.8 = (bf16[1024,1024]{0,1:T(8,128)(2,1)S(1)}, bf16[1024,1024]{0,1:T(8,128)(2,1)}, u32[]{:S(2)}) copy-start(bf16[1024,1024]{0,1:T(8,128)(2,1)} %all-gather.7.cloned.1.call-done) | copy-start | bytes 6291460
  437.6 146.1 %reduce-scatter.3.cloned.1.call-start = ((), (), s32[]{:S(2)}) async-start(), calls=%async_computation.5 | async-start | bytes 2621440 | tf_op jit(solution)/shard_map/reduce_scatter | solution.py:76
  551.4 69.0 %all-gather.9.cloned.1.call-start = ((), (), s32[]{:S(2)}) async-start(), calls=%async_computation.6 | async-start | bytes 2621440 | tf_op jit(solution)/shard_map/all_gather | solution.py:79
  583.7 230.9 %all-reduce.8.cloned.1.call-start = ((), (), s32[]{:S(2)}) async-start(), calls=%async_computation.9 | async-start | bytes 2097152 | tf_op jit(solution)/shard_map/psum | solution.py:14
  622.4 2.7 copy-start
  625.1 1.3 copy-start.2
  627.5 233.9 %reduce-scatter.5.cloned.1.call-start = ((), (), s32[]{:S(2)}) async-start(), calls=%async_computation.7 | async-start | bytes 2359296 | tf_op jit(solution)/shard_map/reduce_scatter | solution.py:27
  628.2 321.3 %all-gather.11.cloned.1.call-start = ((), (), s32[]{:S(2)}) async-start(), calls=%async_computation.8 | async-start | bytes 2359296 | tf_op jit(solution)/shard_map/all_gather | solution.py:28
  814.7 1.7 copy-start.6
  861.4 205.9 %all-reduce.10.cloned.1.call-start = ((), (), s32[]{:S(2)}) async-start(), calls=%async_computation.10 | async-start | bytes 4194304 | tf_op jit(solution)/shard_map/psum | solution.py:14
  949.5 4.1 copy-start.7
  1067.3 5.7 copy-start.1
  1067.3 5.7 copy-start.3
Sparse Core Ops, SparseCore 0:
  10.4 117.2 all-gather.4
  397.6 38.5 all-gather.6
  439.4 106.6 all-reduce.5
  551.5 32.1 reduce-scatter.2
  585.4 34.9 all-gather.8
  627.6 187.0 all-reduce.7
  817.2 41.8 reduce-scatter.4
  861.5 40.6 all-gather.10
  959.0 108.2 all-reduce.9
where the time goes:
time: 1100 us; the launch traced here: 1090 us
  waiting for transfers between devices  611 us (56%)
  other arithmetic  371 us (34%)
  local copies, waits for them, and re-layouts  53.9 us (5%)
  matrix products  37.8 us (3%)
  between operations  17.7 us (2%)
    psum x3, waiting for transfers between devices, spread(): return lax.psum(kept, axis)  394 us
    another operation x16, other arithmetic, local(): factors = jnp.linalg.cholesky(gathered[0])  154 us
    another operation x6, other arithmetic, solve_rows(): lax.linalg.triangular_solve(factor, columns, left_side=False, lower=True,...  119 us
    all_gather x1, waiting for transfers between devices, local(): lax.all_gather(fronts.astype(jnp.bfloat16), ('row', 'col'), axis=3, tiled...  116 us
    another operation x15, other arithmetic, local(): pivot_chol = jnp.linalg.cholesky(pivot_block)  79.1 us
    all_gather x1, waiting for transfers between devices, local(): row_side = lax.all_gather(scaled, 'col', axis=0, tiled=True)  38.6 us
    reduce_scatter x1, waiting for transfers between devices, local(): lax.psum_scatter(update.astype(jnp.bfloat16), 'layer', scatter_dimension=...  32.3 us
    all_gather x1, waiting for transfers between devices, local(): lax.all_gather(shared.astype(jnp.bfloat16), 'layer', axis=0, tiled=True)  29.9 us
  transfers between devices with their start and end apart: 9, of which 7 were waited for; matrix products, arithmetic and copies ran while one was open for 14% of the time, Pallas kernels for 0%

commit v1 on v0

v1 whole, which is shorter than its diff:
```python
import functools
import jax, jax.numpy as jnp
from jax import lax
from jax.experimental import pallas as pl
from jax.experimental.pallas import tpu as pltpu
from jax.sharding import PartitionSpec as P

F32, BF16 = jnp.float32, jnp.bfloat16
N, B, SB = 512, 128, 16

def split(a):
    hi = a.astype(BF16)
    return hi, (a - hi.astype(F32)).astype(BF16)

def dot3(a, b, dims=((1,), (0,))):
    ah, al = a
    bh, bl = b
    d = functools.partial(lax.dot_general, dimension_numbers=(dims, ((), ())), preferred_element_type=F32)
    return d(ah, bh) + (d(al, bh) + d(ah, bl))

def factor_block(dts):
    sub = lax.broadcasted_iota(jnp.int32, (SB, B), 0)
    sub2 = lax.broadcasted_iota(jnp.int32, (SB, 2 * B), 0)
    for s in range(B // SB):
        lo = s * SB
        state = []
        for dt in dts:
            rows = dt[lo:lo + SB, :]
            cols = [jnp.broadcast_to(rows[:, lo + j:lo + j + 1], (SB, B)) for j in range(SB)]
            state.append([rows, cols, []])
        for j in range(SB):
            for st in state:
                g, cols, xs = st
                cj = cols[j]
                d = cj[j:j + 1, :]
                rinv = 1.0 / d
                rs = lax.rsqrt(d)
                row = g[j:j + 1, :]
                xs.append(row * jnp.concatenate([rs, rs], 1))
                rowg = row * jnp.concatenate([rinv, rinv], 1)
                cj2 = jnp.concatenate([cj, cj], 1)
                st[0] = jnp.where(sub2 == j, jnp.broadcast_to(rowg, (SB, 2 * B)), g - cj2 * rowg)
                for k in range(j + 1, SB):
                    ck = cols[k]
                    t = ck[j:j + 1, :] * rinv
                    cols[k] = jnp.where(sub == j, jnp.broadcast_to(t, (SB, B)), ck - cj * t)
        for dt, (g, cols, xs) in zip(dts, state):
            if lo + SB < B:
                rest = slice(lo + SB, B)
                pieces = ([jnp.zeros((lo, 2 * B), F32)] if lo else []) + [g, jnp.zeros((B - lo - SB, 2 * B), F32)]
                pad = jnp.concatenate(pieces, 0)
                dt[rest, :] = dt[rest, :] - dot3(split(dt[rest, 0:B]), split(pad))
            dt[lo:lo + SB, :] = jnp.concatenate(xs, 0)

def chol_steps(a_refs, y_refs, dts, xrs):
    n = len(a_refs)
    eye = (lax.broadcasted_iota(jnp.int32, (B, B), 0) == lax.broadcasted_iota(jnp.int32, (B, B), 1)).astype(F32)
    for y in y_refs:
        y[...] = jnp.zeros((N, N), F32)
    for k in range(N // B):
        for y in y_refs:
            y[k * B:(k + 1) * B, k * B:(k + 1) * B] = eye

    def outer(k, _):
        o = pl.multiple_of(k * B, B)
        blk = pl.ds(o, B)
        for a, dt in zip(a_refs, dts):
            dt[:, 0:B] = a[blk, blk]
            dt[:, B:2 * B] = eye
        factor_block(dts)
        for a, y, dt, xr in zip(a_refs, y_refs, dts, xrs):
            t = split(dt[:, B:2 * B])
            xr[:, 0:N] = dot3(t, split(a[blk, :]))
            yk = dot3(t, split(y[blk, :]))
            xr[:, N:2 * N] = yk
            y[blk, :] = yk

        def inner(i, _):
            oi = pl.multiple_of(i * B, B)
            bi = pl.ds(oi, B)
            for a, y, xr in zip(a_refs, y_refs, xrs):
                up = dot3(split(xr[:, bi]), split(xr[...]), ((0,), (0,)))
                a[bi, :] = a[bi, :] - up[:, 0:N]
                y[bi, :] = y[bi, :] - up[:, N:2 * N]
            return 0
        lax.fori_loop(k + 1, N // B, inner, 0)
        return 0
    lax.fori_loop(0, N // B, outer, 0)

def fronts_kernel(g, out_ref, *scr):
    a, y, dt, xr = (scr[i * 2:(i + 1) * 2] for i in range(4))

    def move(r, _):
        for zh in range(4):
            for core in range(2):
                rows = pl.ds(pl.multiple_of(64 * r + 16 * zh + 8 * core, 8), 8)
                for p in range(2):
                    a[p][rows, :] = g[r, zh, core, p].astype(F32)
        return 0

    lax.fori_loop(0, 8, move, 0)
    chol_steps(a, y, dt, xr)
    for p in range(2):
        out_ref[p] = y[p][...].astype(BF16)


def pivot_chol_kernel(x, out_ref, a, dt, xr):
    a[...] = x[...]
    chol_steps([a], [out_ref], [dt], [xr])


def chol_scratch(nb, y=True):
    return (
        [pltpu.VMEM((N, N), F32)] * (nb * (1 + y)) + [pltpu.VMEM((B, 2 * B), F32)] * nb + [pltpu.VMEM((B, 2 * N), F32)] * nb
    )


def chol_call(kernel, x, shape, dtype, scratch, flops):
    vm = pl.BlockSpec(memory_space=pltpu.VMEM)
    return pl.pallas_call(
        kernel,
        out_shape=jax.ShapeDtypeStruct(shape, dtype),
        in_specs=[vm],
        out_specs=vm,
        scratch_shapes=scratch,
        cost_estimate=pl.CostEstimate(flops=flops, bytes_accessed=2_000_000, transcendentals=0),
    )(x)


def chol_fronts(g):
    return chol_call(fronts_kernel, g, (2, N, N), BF16, chol_scratch(2), 400_000_000)


def chol_pivot(x):
    return chol_call(pivot_chol_kernel, x, (N, N), F32, chol_scratch(1, False), 300_000_000)


MESH = pl.DeviceIdType.MESH
VM = pltpu.VMEM


class Place:
    def __init__(self):
        self.l, self.r, self.c = (lax.axis_index(a) for a in ("layer", "row", "col"))
        self.x, self.zl = self.r // 2, self.r % 2
        self.zh, self.core = self.c // 2, self.c % 2
        self.z = 2 * self.zh + self.zl
        self.partner = {"col": 2 * self.zh + 1 - self.core}

    def along_z(self, k):
        z = (self.z + k) % 8
        return {"row": 2 * self.x + z % 2, "col": 2 * (z // 2) + self.core}

    def along_x(self, k):
        return {"row": 2 * ((self.x + k) % 4) + self.zl}


class Copies:
    def __init__(self, send, recv):
        self.send, self.recv, self.used, self.open = send, recv, 0, []

    def new(self, src, dst, device, when=None):
        i = self.used
        self.used += 1
        copy = pltpu.make_async_remote_copy(
            src_ref=src, dst_ref=dst, send_sem=self.send.at[i], recv_sem=self.recv.at[i],
            device_id=device, device_id_type=MESH,
        )
        if when is None:
            copy.start()
        else:
            pl.when(when)(copy.start)
        self.open.append((copy, when))
        return copy

    def drain(self):
        for copy, when in self.open:
            if when is None:
                copy.wait_send()
            else:
                pl.when(when)(copy.wait_send)


class Spread64:
    def __init__(self, at, copies, buf):
        self.at, self.copies, self.buf = at, copies, buf

    def first(self, src):
        at = self.at
        slot = self.buf.at[at.r, at.zh, at.core]
        self.a = [self.copies.new(src, slot, at.along_z(k)) for k in range(1, 8)]

    def second(self):
        at = self.at
        for copy in self.a:
            copy.wait_recv()
        part = self.buf.at[pl.ds(2 * at.x, 2), :, at.core]
        self.b = [self.copies.new(part, part, at.along_x(k)) for k in range(1, 4)]

    def third(self):
        for copy in self.b:
            copy.wait_recv()
        part = self.buf.at[:, :, self.at.core]
        self.d = self.copies.new(part, part, self.at.partner)

    def last(self):
        self.d.wait_recv()


class Blocks:
    def __init__(self, at, copies, rows, cols):
        self.at, self.copies, self.rows, self.cols = at, copies, rows, cols

    def first(self, src):
        at, new = self.at, self.copies.new
        self.off = at.r != at.c
        self.perm = new(src, self.cols.at[at.c], {"row": at.c, "col": at.r}, self.off)
        mine = self.rows.at[at.c]
        self.own = new(src, mine, at.partner)
        self.b = [new(src, mine, {"col": 2 * ((at.zh + k) % 4) + at.core}) for k in range(1, 4)]

    def second(self):
        at, new = self.at, self.copies.new
        pl.when(self.off)(self.perm.wait_recv)
        mine = self.cols.at[at.r]
        self.zl = new(mine, mine, {"row": 2 * at.x + 1 - at.zl})
        self.xo = [new(mine, mine, at.along_x(k)) for k in range(1, 4)]

    def third(self):
        at, new = self.at, self.copies.new
        self.zl.wait_recv()
        other = self.cols.at[2 * at.x + 1 - at.zl]
        self.xp = [new(other, other, at.along_x(k)) for k in range(1, 4)]

    def fourth(self):
        at, new = self.at, self.copies.new
        self.fwd = []
        for k in range(1, 4):
            self.b[k - 1].wait_recv()
            slot = self.rows.at[2 * ((at.zh + 4 - k) % 4) + at.core]
            self.fwd.append(new(slot, slot, at.partner))

    def last(self):
        for copy in [self.own, *self.xo, *self.xp, *self.fwd]:
            copy.wait_recv()


def scatter16(at, piece, buf, send, recv):
    source = (at.r == 0) & (at.c < 4)

    def copy(i):
        row, col = 2 * at.c + i // 8, i % 8
        return pltpu.make_async_remote_copy(
            src_ref=piece(i), dst_ref=buf.at[row, col // 2, col % 2], send_sem=send.at[i], recv_sem=recv.at[0],
            device_id={"row": row, "col": col}, device_id_type=MESH,
        )

    def to_all(act):
        def step(i, _):
            pl.when((at.c > 0) | (i > 0))(lambda: act(copy(i)))
            return 0

        lax.fori_loop(0, 16, step, 0)

    start = lambda: to_all(lambda one: one.start())
    done = lambda: to_all(lambda one: one.wait_send())
    pl.when(source)(start)
    is_zero = (at.r == 0) & (at.c == 0)

    def arrived():
        slot = buf.at[at.r, at.zh, at.core]
        pl.when(jnp.logical_not(is_zero))(
            pltpu.make_async_remote_copy(
                src_ref=slot, dst_ref=slot, send_sem=send.at[0], recv_sem=recv.at[0],
                device_id=at.partner, device_id_type=MESH,
            ).wait_recv
        )

    return arrived, lambda: pl.when(source)(done)


def inputs_kernel(fr, m, m16, anc, g, mr, mc, g0, own_a, send, recv, s16, r16, sa, ra, la):
    at = Place()
    copies = Copies(send, recv)
    fronts, lead, blocks = Spread64(at, copies, g), Spread64(at, copies, g0), Blocks(at, copies, mr, mc)
    here = at.zh == at.l

    def handed(e):
        rows = pl.ds(pl.multiple_of(256 * at.l + 128 * e, 128), 128)
        return pltpu.make_async_remote_copy(
            src_ref=anc.at[rows, pl.ds(0, 512)], dst_ref=own_a, send_sem=sa.at[e], recv_sem=ra.at[0],
            device_id={"col": 2 * at.l + e}, device_id_type=MESH,
        )

    def kept():
        return pltpu.make_async_copy(anc.at[pl.ds(0, 128), pl.ds(0, 512)], own_a, la)

    fronts.first(fr)
    arrived, scattered = scatter16(at, lambda i: m16.at[i], g0, s16, r16)
    blocks.first(m)
    corner = (at.c == 0) & (at.l == 0)
    pl.when((at.c == 0) & (at.l > 0))(handed(0).start)
    pl.when(at.c == 0)(handed(1).start)
    pl.when(corner)(lambda: kept().start())
    g[at.r, at.zh, at.core] = fr[...]
    mr[at.c] = m[...]

    @pl.when(at.r == at.c)
    def _():
        mc[at.r] = m[...]

    @pl.when((at.r == 0) & (at.c == 0))
    def _():
        g0[0, 0, 0] = m16[0]

    fronts.second()
    blocks.second()
    arrived()
    lead.first(g0.at[at.r, at.zh, at.core])
    fronts.third()
    blocks.third()
    lead.second()

    def over_y(k):
        return pltpu.make_async_remote_copy(
            src_ref=own_a, dst_ref=own_a, send_sem=sa.at[1 + k], recv_sem=ra.at[1],
            device_id={"layer": (at.l + k) % 4}, device_id_type=MESH,
        )

    pl.when(corner)(lambda: kept().wait())
    pl.when(here & jnp.logical_not(corner))(handed(0).wait_recv)

    @pl.when(here)
    def _():
        for k in range(1, 4):
            over_y(k).start()

    blocks.fourth()
    lead.third()
    fronts.last()
    blocks.last()
    lead.last()
    pl.when(jnp.logical_not(here))(over_y(1).wait_recv)

    @pl.when(here)
    def _():
        for k in range(1, 4):
            over_y(k).wait_send()

    pl.when((at.c == 0) & (at.l > 0))(handed(0).wait_send)
    pl.when(at.c == 0)(handed(1).wait_send)
    copies.drain()
    scattered()


def sems(n):
    return pltpu.SemaphoreType.DMA((n,))


def gather_inputs(fr, m, anc):
    s = jax.ShapeDtypeStruct
    vm = pl.BlockSpec(memory_space=VM)
    return pl.pallas_call(
        inputs_kernel,
        out_shape=[
            s((8, 4, 2, 2, 8, 512), BF16), s((8, 128, 1024), BF16), s((8, 128, 1024), BF16),
            s((8, 4, 2, 8, 1024), BF16), s((128, 512), F32),
        ],
        in_specs=[vm, vm, vm, pl.BlockSpec(memory_space=pl.ANY)],
        out_specs=[vm] * 5,
        scratch_shapes=[sems(40), sems(40), sems(16), sems(1), sems(5), sems(2), pltpu.SemaphoreType.DMA],
        compiler_params=pltpu.CompilerParams(has_side_effects=True),
    )(fr, m, m.reshape(16, 8, 1024), anc)


def pivot_kernel(q, own_a, lead, gp, cr, cc, parts, send, recv, s16, r16, sy, ry):
    at = Place()
    copies = Copies(send, recv)
    ys = []
    for k in range(1, 4):
        ys.append(pltpu.make_async_remote_copy(
            src_ref=q, dst_ref=parts.at[at.l], send_sem=sy.at[k - 1], recv_sem=ry.at[k - 1],
            device_id={"layer": (at.l + k) % 4}, device_id_type=MESH,
        ))
        ys[-1].start()
    parts[at.l] = q[...]
    for copy in ys:
        copy.wait_recv()
    lead[...] = own_a[...] - (((parts[0] + parts[1]) + parts[2]) + parts[3])
    spread, blocks = Spread64(at, copies, gp), Blocks(at, copies, cr, cc)
    arrived, scattered = scatter16(at, lambda i: lead.at[pl.ds(pl.multiple_of(8 * i, 8), 8)], gp, s16, r16)
    cr[at.c] = lead[...]

    @pl.when(at.r == at.c)
    def _():
        cc[at.r] = lead[...]

    @pl.when((at.r == 0) & (at.c == 0))
    def _():
        gp[0, 0, 0] = lead[0:8, :]

    arrived()
    spread.first(gp.at[at.r, at.zh, at.core])
    blocks.first(lead)
    spread.second()
    blocks.second()
    spread.third()
    blocks.third()
    blocks.fourth()
    spread.last()
    blocks.last()
    copies.drain()
    scattered()
    for copy in ys:
        copy.wait_send()


def gather_pivot(q, own_a):
    s = jax.ShapeDtypeStruct
    vm = pl.BlockSpec(memory_space=VM)
    return pl.pallas_call(
        pivot_kernel,
        out_shape=[s((128, 512), F32), s((8, 4, 2, 8, 512), F32), s((8, 128, 512), F32), s((8, 128, 512), F32)],
        in_specs=[vm, vm],
        out_specs=[vm] * 4,
        scratch_shapes=[pltpu.VMEM((4, 128, 512), F32), sems(30), sems(30), sems(16), sems(1), sems(3), sems(3)],
        compiler_params=pltpu.CompilerParams(has_side_effects=True),
        cost_estimate=pl.CostEstimate(flops=200_000_000, bytes_accessed=8_000_000, transcendentals=0),
    )(q, own_a)


def local(ancestor, coupling, fronts, tile_pattern):
    r, c = lax.axis_index("row"), lax.axis_index("col")
    fr = jnp.swapaxes(fronts[0], 1, 2).astype(BF16)
    on = lax.dynamic_slice_in_dim(tile_pattern[0], r, 1, 1)
    masked = coupling[0] * jnp.repeat(on[:, 0], 512)[None, :].astype(BF16)
    g, mr, mc, m0, own_a = gather_inputs(fr, masked, ancestor)
    inv = chol_fronts(g)

    def solved(rows):
        out = [
            lax.dot_general(rows[:, p * 512:(p + 1) * 512], inv[p], (((1,), (1,)), ((), ())), preferred_element_type=F32)
            for p in range(2)
        ]
        return jnp.concatenate(out, 1).astype(BF16)

    outer = lambda a, b: lax.dot_general(a, b, (((1,), (1,)), ((), ())), preferred_element_type=F32)
    q = outer(solved(masked), solved(m0.reshape(512, 1024)))
    row_side, col_side = solved(mr.reshape(1024, 1024)), solved(mc.reshape(1024, 1024))
    update = outer(row_side, col_side).astype(BF16)
    share = lax.psum_scatter(update, "layer", scatter_dimension=0, tiled=True)
    summed = lax.all_gather(share, "layer", axis=0, tiled=True)
    lead, gp, cr, cc = gather_pivot(q, own_a)
    pinv = chol_pivot(gp.reshape(512, 512))
    high = functools.partial(
        lax.dot_general, dimension_numbers=(((1,), (1,)), ((), ())), precision=lax.Precision.HIGH, preferred_element_type=F32
    )
    rows = high(cr.reshape(1024, 512), pinv)
    cols = high(cc.reshape(1024, 512), pinv)
    schur = ancestor - summed.astype(F32) - high(rows, cols)
    panel = high(lead, pinv)
    scale = jnp.diagonal(lax.dynamic_slice(pinv, (8 * (8 * r + c), 0), (8, 512)).reshape(8, 64, 8)[:, 8 * r + c])
    return schur, panel, 1.0 / (scale * scale)


def solution(mesh):
    return jax.shard_map(
        local,
        mesh=mesh,
        in_specs=(
            P("row", "col"),
            P("layer", ("row", "col"), None),
            P("layer", None, None, ("row", "col")),
            P("layer", None, None),
        ),
        out_specs=(P("row", "col"), P(("row", "col"), None), P(("row", "col"))),
        check_vma=False,
    )
```

time: 1100 us -> 318 us (0.29)
  waiting for transfers between devices: 611 us -> 36.7 us
  other arithmetic: 371 us -> 6.11 us
  Pallas kernels: 0 us -> 229 us
  local copies, waits for them, and re-layouts: 53.9 us -> 2.55 us
    psum x3 -> x0, waiting for transfers between devices: 394 us -> none  [spread(): return lax.psum(kept, axis)]
    another operation x39 -> x0, other arithmetic: 352 us -> none  [the longest x16 154 us: local(): factors = jnp.linalg.cholesky(gathered[0])]
    pallas_call x0 -> x4, Pallas kernels: none -> 229 us  [the longest x1 101 us: gather_pivot(): pl.pallas_call(pivot_kernel, out_shape=[s((128, 512), F32), s((8, 4, 2, 8...]
    all_gather x4 -> x1, waiting for transfers between devices: 184 us -> 0.01 us  [local(): summed = lax.all_gather(share, 'layer', axis=0, tiled=True)]
    another operation x65 -> x0, local copies, waits for them, and re-layouts: 25.8 us -> none  [the longest x28 16.8 us: solve_rows(): lax.linalg.triangular_solve(factor, columns, left_side=False, lower=True,...]
    another operation x33 -> x0, matrix products: 20.9 us -> none  [the longest x21 11.9 us: solve_rows(): lax.linalg.triangular_solve(factor, columns, left_side=False, lower=True,...]
    unnamed x26 -> x18, local copies, waits for them, and re-layouts: 13.9 us -> 0.94 us
    dot_general x4 -> x14, matrix products: 16.9 us -> 27.5 us  [the longest x1 7.63 us: local(): schur = ancestor - summed.astype(F32) - high(rows, cols)]
  transfers between devices with their start and end apart: 9 -> 2, of which waited for: 7 -> 1; matrix products, arithmetic and copies ran while one was open for 14% -> 4% of each run, Pallas kernels for 0% -> 38%
where the time goes in v1:
time: 318 us; the launch traced here: 316 us
  Pallas kernels  229 us (72%)
  waiting for transfers between devices  36.7 us (12%)
  matrix products  27.5 us (9%)
  between operations  14.2 us (4%)
  other arithmetic  6.11 us (2%)
    pallas_call x1, Pallas kernels, gather_pivot(): pl.pallas_call(pivot_kernel, out_shape=[s((128, 512), F32), s((8, 4, 2, 8...  101 us
    pallas_call x1, Pallas kernels, gather_inputs(): pl.pallas_call(inputs_kernel, out_shape=[s((8, 4, 2, 2, 8, 512), BF16), s...  84.1 us
    pallas_call x2, Pallas kernels, chol_call(): pl.pallas_call(kernel, out_shape=jax.ShapeDtypeStruct(shape, dtype), in_s...  44 us
    reduce_scatter x1, waiting for transfers between devices, local(): share = lax.psum_scatter(update, 'layer', scatter_dimension=0, tiled=True)  36.7 us
    dot_general x1, matrix products, local(): schur = ancestor - summed.astype(F32) - high(rows, cols)  7.63 us
  transfers between devices with their start and end apart: 2, of which 1 were waited for; matrix products, arithmetic and copies ran while one was open for 4% of the time, Pallas kernels for 38%

profile of v1, /device:TPU:1, one launch (start us, length us, event | category | flops | bytes accessed | tf_op | source)
XLA Modules:
  0.0 316.2 jit_solution(5325754846594568475)
XLA Ops:
  7.2 0.0 reduce-scatter.2.cloned.1.call-start
  7.2 0.9 fusion.27
  8.1 0.1 broadcast_bitcast_fusion
  8.2 1.7 bitcast_multiply_fusion.1.m
  9.8 1.7 bitcast_multiply_fusion.m16
  11.5 1.4 convert_bitcast_fusion.fr
  12.9 84.1 %shard_map.67 = (bf16[8,4,2,2,8,512]{5,4,3,2,1,0:T(8,128)(2,1)}, bf16[8,128,1024]{2,1,0:T(8,128)(2,1)}, bf16[8,128,1024]{2,1,0:T(8,128)(2,1)}, bf16[8,4,2,8,1024]{4,3,2,1,0:T(8,128)(2,1)}, f32[128,512]{1,0:T(8,128)}) custom-call(bf16[2,8,512]{2,1,0:T(8,128)(2,1)} %convert_bitcast_fusion.fr, bf16[128,1024]{1,0:T(8,128)(2,1)} %bitcast_multiply_fusion.1.m, ...), custom_call_target="tpu_custom_call" | custom-call | tf_op jit(solution)/shard_map/pallas_call | solution.py:363
  97.0 0.0 copy-start.6
  97.0 24.8 %shard_map.68 = bf16[2,512,512]{2,1,0:T(8,128)(2,1)} custom-call(bf16[8,4,2,2,8,512]{5,4,3,2,1,0:T(8,128)(2,1)} %get-tuple-element.13.g), custom_call_target="tpu_custom_call" | custom-call | flops 400000000 | bytes 2000000 | tf_op jit(solution)/shard_map/pallas_call | solution.py:120
  121.8 0.0 copy-start.3
  121.8 0.0 copy-done.6
  121.8 1.9 convolution_convert_fusion
  123.7 0.0 copy-done.3
  123.7 0.0 copy-start.5
  123.7 0.7 convolution_convert_fusion.1
  124.5 0.8 copy-done.5
  125.3 0.7 convolution_convert_fusion.2
  126.0 0.7 convolution_convert_fusion.3
  126.8 3.7 %fusion.7 = bf16[1024,1024]{1,0:T(8,128)(2,1)} fusion(bf16[1024,512]{1,0:T(8,128)(2,1)S(1)} %convolution_convert_fusion, bf16[1024,512]{1,0:T(8,128)(2,1)S(1)} %convolution_convert_fusion.1, bf16[1024,512]{1,0:T(8,128)(2,1)S(1)} %convolution_convert_fusion.2, bf16[1024,512]{1,0:T(8,128)(2,1)S(1)} %convolution_convert_fusion.3), kind=kOutput, calls=%fused_computation.9 | convolution fusion | flops 2156920832 | bytes 6291456 | tf_op jit(solution)/shard_map/dot_general | solution.py:447
  130.5 0.0 copy-start.2
  130.5 0.0 copy-start.7
  130.5 0.0 reduce-scatter.2.cloned.1.call-update
  130.5 0.0 all-gather.2.cloned.1.call-start
  130.6 36.7 %reduce-scatter.2.cloned.1.call-done = bf16[256,1024]{1,0:T(8,128)(2,1)} async-done(((bf16[1024,1024]{1,0:T(8,128)(2,1)}), bf16[256,1024]{1,0:T(8,128)(2,1)}) %reduce-scatter.2.cloned.1.call-update) | async-done | bytes 524304 | tf_op jit(solution)/shard_map/reduce_scatter | solution.py:451
  167.2 0.0 all-gather.2.cloned.1.call-update
  167.2 0.0 copy-done.2
  167.3 0.3 convolution_convert_fusion.6
  167.6 0.3 convolution_convert_fusion.7
  167.9 0.0 copy-done.7
  167.9 0.5 convolution_convert_fusion.4
  168.4 0.5 convolution_convert_fusion.5
  168.8 1.2 fusion.16.q
  170.0 101.0 %shard_map.69 = (f32[128,512]{1,0:T(8,128)}, f32[8,4,2,8,512]{4,3,2,1,0:T(8,128)}, f32[8,128,512]{2,1,0:T(8,128)}, f32[8,128,512]{2,1,0:T(8,128)}) custom-call(f32[128,512]{1,0:T(8,128)} %fusion.16.q, f32[128,512]{1,0:T(8,128)} %get-tuple-element.16.own_a), custom_call_target="tpu_custom_call" | custom-call | flops 200000000 | bytes 8000000 | tf_op jit(solution)/shard_map/pallas_call | solution.py:421
  271.0 0.0 copy-start.4
  271.0 19.1 %shard_map.70 = f32[512,512]{1,0:T(8,128)} custom-call(f32[512,512]{1,0:T(8,128)} %bitcast.43), custom_call_target="tpu_custom_call" | custom-call | flops 300000000 | bytes 2000000 | tf_op jit(solution)/shard_map/pallas_call | solution.py:120
  290.1 0.0 copy-start
  290.1 0.8 constant_dynamic-slice_fusion.1
  291.0 0.2 reshape.52
  291.2 0.6 gather_fusion
  291.8 0.5 multiply_divide_fusion
  292.3 0.0 copy-done.4
  292.3 2.6 fusion.32
  294.9 0.0 copy-done
  294.9 0.0 copy-start.1
  294.9 3.6 %fusion.30 = f32[1024,512]{1,0:T(8,128)S(1)} fusion(f32[1024,512]{1,0:T(8,128)} %bitcast.42, f32[512,512]{1,0:T(8,128)S(1)} %copy-done), kind=kOutput, calls=%fused_computation.47 | convolution fusion | flops 1610612736 | bytes 5242880 | tf_op jit(solution)/shard_map/dot_general | solution.py:458
  298.5 0.0 copy-done.1
  298.5 3.2 %fusion.31 = f32[1024,512]{1,0:T(8,128)} fusion(f32[1024,512]{1,0:T(8,128)S(1)} %bitcast.41, f32[512,512]{1,0:T(8,128)S(1)} %copy-done), kind=kOutput, calls=%fused_computation.48 | convolution fusion | flops 1610612736 | bytes 5242880 | tf_op jit(solution)/shard_map/dot_general | solution.py:459
  301.7 0.0 all-gather.2.cloned.1.call-done
  301.7 7.6 %subtract_subtract_fusion = f32[1024,1024]{1,0:T(8,128)} fusion(f32[1024,1024]{1,0:T(8,128)} %anc.1, bf16[1024,1024]{1,0:T(8,128)(2,1)} %all-gather.2.cloned.1.call-done, f32[1024,512]{1,0:T(8,128)S(1)} %fusion.30, f32[1024,512]{1,0:T(8,128)} %fusion.31), kind=kOutput, calls=%fused_computation.1 | convolution fusion | flops 3224371200 | bytes 14680064 | tf_op jit(solution)/shard_map/dot_general | solution.py:460
  (3 shorter events, 0.0 us)
Async XLA Ops:
  7.2 160.0 %reduce-scatter.2.cloned.1.call-start = ((), (), s32[]{:S(2)}) async-start(), calls=%async_computation.1 | async-start | bytes 2621440 | tf_op jit(solution)/shard_map/reduce_scatter | solution.py:451
  97.0 24.8 %copy-start.6 = (bf16[8,128,1024]{2,1,0:T(8,128)(2,1)S(1)}, bf16[8,128,1024]{2,1,0:T(8,128)(2,1)}, u32[]{:S(2)}) copy-start(bf16[8,128,1024]{2,1,0:T(8,128)(2,1)} %get-tuple-element.14) | copy-start | bytes 6291460
  121.8 1.9 copy-start.3
  123.7 1.6 copy-start.5
  130.5 36.8 %copy-start.2 = (bf16[128,1024]{1,0:T(8,128)(2,1)S(1)}, bf16[128,1024]{1,0:T(8,128)(2,1)}, u32[]{:S(2)}) copy-start(bf16[128,1024]{1,0:T(8,128)(2,1)} %bitcast_multiply_fusion.1.m) | copy-start | bytes 786436
  130.5 37.4 %copy-start.7 = (bf16[8,4,2,8,1024]{4,3,2,1,0:T(8,128)(2,1)S(1)}, bf16[8,4,2,8,1024]{4,3,2,1,0:T(8,128)(2,1)}, u32[]{:S(2)}) copy-start(bf16[8,4,2,8,1024]{4,3,2,1,0:T(8,128)(2,1)} %get-tuple-element.15) | copy-start | bytes 3145732
  130.5 171.2 %all-gather.2.cloned.1.call-start = ((), (), s32[]{:S(2)}) async-start(), calls=%async_computation.2 | async-start | bytes 2621440 | tf_op jit(solution)/shard_map/all_gather | solution.py:452
  271.0 21.3 %copy-start.4 = (f32[128,512]{1,0:T(8,128)S(1)}, f32[128,512]{1,0:T(8,128)}, u32[]{:S(2)}) copy-start(f32[128,512]{1,0:T(8,128)} %get-tuple-element.20) | copy-start | bytes 786436
  290.1 4.8 %copy-start = (f32[512,512]{1,0:T(8,128)S(1)}, f32[512,512]{1,0:T(8,128)}, u32[]{:S(2)}) copy-start(f32[512,512]{1,0:T(8,128)} %shard_map.70) | copy-start | bytes 3145732
  294.9 3.6 %copy-start.1 = (f32[8,128,512]{2,1,0:T(8,128)S(1)}, f32[8,128,512]{2,1,0:T(8,128)}, u32[]{:S(2)}) copy-start(f32[8,128,512]{2,1,0:T(8,128)} %get-tuple-element.19) | copy-start | bytes 6291460
Sparse Core Ops, SparseCore 0:
  130.6 36.5 reduce-scatter.1
  169.0 43.9 all-gather.1

commit v2 on v1

v2 whole, which is shorter than its diff:
```python
import functools
import jax, jax.numpy as jnp
from jax import lax
from jax.experimental import pallas as pl
from jax.experimental.pallas import tpu as pltpu
from jax.sharding import PartitionSpec as P

F32, BF16 = jnp.float32, jnp.bfloat16
N, B, SB = 512, 128, 16

def split(a):
    hi = a.astype(BF16)
    return hi, (a - hi.astype(F32)).astype(BF16)

def dot3(a, b, dims=((1,), (0,))):
    ah, al = a
    bh, bl = b
    d = functools.partial(lax.dot_general, dimension_numbers=(dims, ((), ())), preferred_element_type=F32)
    return d(ah, bh) + (d(al, bh) + d(ah, bl))

def factor_block(dts):
    sub = lax.broadcasted_iota(jnp.int32, (SB, B), 0)
    sub2 = lax.broadcasted_iota(jnp.int32, (SB, 2 * B), 0)
    for s in range(B // SB):
        lo = s * SB
        state = []
        for dt in dts:
            rows = dt[lo:lo + SB, :]
            cols = [jnp.broadcast_to(rows[:, lo + j:lo + j + 1], (SB, B)) for j in range(SB)]
            state.append([rows, cols, []])
        for j in range(SB):
            for st in state:
                g, cols, xs = st
                cj = cols[j]
                d = cj[j:j + 1, :]
                rinv = 1.0 / d
                rs = lax.rsqrt(d)
                row = g[j:j + 1, :]
                xs.append(row * jnp.concatenate([rs, rs], 1))
                rowg = row * jnp.concatenate([rinv, rinv], 1)
                cj2 = jnp.concatenate([cj, cj], 1)
                st[0] = jnp.where(sub2 == j, jnp.broadcast_to(rowg, (SB, 2 * B)), g - cj2 * rowg)
                for k in range(j + 1, SB):
                    ck = cols[k]
                    t = ck[j:j + 1, :] * rinv
                    cols[k] = jnp.where(sub == j, jnp.broadcast_to(t, (SB, B)), ck - cj * t)
        for dt, (g, cols, xs) in zip(dts, state):
            if lo + SB < B:
                rest = slice(lo + SB, B)
                pieces = ([jnp.zeros((lo, 2 * B), F32)] if lo else []) + [g, jnp.zeros((B - lo - SB, 2 * B), F32)]
                pad = jnp.concatenate(pieces, 0)
                dt[rest, :] = dt[rest, :] - dot3(split(dt[rest, 0:B]), split(pad))
            dt[lo:lo + SB, :] = jnp.concatenate(xs, 0)

def chol_steps(a_refs, y_refs, dts, xrs, stages=()):
    n = len(a_refs)
    eye = (lax.broadcasted_iota(jnp.int32, (B, B), 0) == lax.broadcasted_iota(jnp.int32, (B, B), 1)).astype(F32)
    for y in y_refs:
        y[...] = jnp.zeros((N, N), F32)
    for k in range(N // B):
        for y in y_refs:
            y[k * B:(k + 1) * B, k * B:(k + 1) * B] = eye

    def outer(k, _):
        o = pl.multiple_of(k * B, B)
        blk = pl.ds(o, B)
        for a, dt in zip(a_refs, dts):
            dt[:, 0:B] = a[blk, blk]
            dt[:, B:2 * B] = eye
        factor_block(dts)
        for a, y, dt, xr in zip(a_refs, y_refs, dts, xrs):
            t = split(dt[:, B:2 * B])
            xr[:, 0:N] = dot3(t, split(a[blk, :]))
            yk = dot3(t, split(y[blk, :]))
            xr[:, N:2 * N] = yk
            y[blk, :] = yk

        def inner(i, _):
            oi = pl.multiple_of(i * B, B)
            bi = pl.ds(oi, B)
            for a, y, xr in zip(a_refs, y_refs, xrs):
                up = dot3(split(xr[:, bi]), split(xr[...]), ((0,), (0,)))
                a[bi, :] = a[bi, :] - up[:, 0:N]
                y[bi, :] = y[bi, :] - up[:, N:2 * N]
            return 0
        lax.fori_loop(k + 1, N // B, inner, 0)
        for i, stage in enumerate(stages):
            pl.when(k == i)(stage)
        return 0
    lax.fori_loop(0, N // B, outer, 0)

def chol_scratch(nb, y=True):
    return (
        [pltpu.VMEM((N, N), F32)] * (nb * (1 + y)) + [pltpu.VMEM((B, 2 * B), F32)] * nb + [pltpu.VMEM((B, 2 * N), F32)] * nb
    )


MESH = pl.DeviceIdType.MESH
VM = pltpu.VMEM
WHOLE, LOW, HIGH = pl.ds(0, 128), pl.ds(0, 64), pl.ds(64, 64)


class Place:
    def __init__(self):
        self.l, self.r, self.c = (lax.axis_index(a) for a in ("layer", "row", "col"))
        self.x, self.zl = self.r // 2, self.r % 2
        self.zh, self.core = self.c // 2, self.c % 2
        self.z = 2 * self.zh + self.zl
        self.d = 8 * self.r + self.c
        self.partner = {"col": 2 * self.zh + 1 - self.core}
        self.mirror = {"row": self.c, "col": self.r}
        self.off = self.r != self.c

    def along_z(self, k):
        z = (self.z + k) % 8
        return {"row": 2 * self.x + z % 2, "col": 2 * (z // 2) + self.core}

    def along_x(self, k):
        return {"row": 2 * ((self.x + k) % 4) + self.zl}

    def along_y(self, k):
        return {"layer": (self.l + k) % 4}


class Copies:
    def __init__(self, send, recv):
        self.send, self.recv, self.all = send, recv, []

    def new(self, src, dst, device, when=None):
        i = len(self.all)
        self.all.append((pltpu.make_async_remote_copy(
            src_ref=src, dst_ref=dst, send_sem=self.send.at[i], recv_sem=self.recv.at[i],
            device_id=device, device_id_type=MESH,
        ), when))
        return self.all[-1]

    def drain(self):
        for copy, when in self.all:
            act(when, copy.wait_send)


def act(when, f):
    if when is None:
        f()
    else:
        pl.when(when)(f)


def start(*copies):
    for copy, when in copies:
        act(when, copy.start)


def arrive(*copies):
    for copy, when in copies:
        act(when, copy.wait_recv)


def meet(at, extra=()):
    barrier = pltpu.get_barrier_semaphore()

    def greet(device):
        pl.semaphore_signal(barrier, inc=1, device_id=device, device_id_type=MESH)

    for k in range(1, 8):
        greet(at.along_z(k))
    for k in range(1, 4):
        greet(at.along_x(k))
        greet(at.along_y(k))
    greet(at.partner)
    pl.when(at.off)(lambda: greet(at.mirror))
    total = 14 + at.off.astype(jnp.int32)
    for when, device in extra:
        pl.when(when)(functools.partial(greet, device))
        total = total + when.astype(jnp.int32)
    return barrier, greet, total


class Spread64:
    def __init__(self, at, copies, buf, src):
        slot = buf.at[at.r, at.zh, at.core]
        self.a = [copies.new(src, slot, at.along_z(k)) for k in range(1, 8)]
        part = buf.at[pl.ds(2 * at.x, 2), :, at.core]
        self.b = [copies.new(part, part, at.along_x(k)) for k in range(1, 4)]
        part = buf.at[:, :, at.core]
        self.d = [copies.new(part, part, at.partner)]

    def first(self):
        start(*self.a)

    def second(self):
        arrive(*self.a)
        start(*self.b)

    def third(self):
        arrive(*self.b)
        start(*self.d)

    def last(self):
        arrive(*self.d)


class Blocks:
    def __init__(self, at, copies, rows, cols, src):
        new = copies.new
        up, down = {"col": 2 * ((at.zh + 1) % 4) + at.core}, {"col": 2 * ((at.zh + 3) % 4) + at.core}
        mine = rows.at[at.c]
        below, above = 2 * ((at.zh + 3) % 4) + at.core, 2 * ((at.zh + 1) % 4) + at.core
        far = 2 * ((at.zh + 2) % 4) + at.core
        self.perm = new(src, cols.at[at.c], at.mirror, at.off)
        self.b = [new(src, mine, up), new(src, mine, down)]
        self.own = new(src, mine, at.partner)
        half = lambda ref, s, h, dev: new(ref.at[s, h], ref.at[s, h], dev)
        self.bfar = [half(rows, below, LOW, up), half(rows, above, HIGH, down)]
        self.fwd = [half(rows, s, WHOLE, at.partner) for s in (below, above)]
        self.fwdfar = half(rows, far, WHOLE, at.partner)
        self.zl = half(cols, at.r, WHOLE, {"row": 2 * at.x + 1 - at.zl})
        self.near, self.relay = [], []
        for zl in (at.zl, 1 - at.zl):
            here, left, right = (2 * ((at.x + k) % 4) + zl for k in (0, 3, 1))
            self.near.append([half(cols, here, WHOLE, at.along_x(k)) for k in (1, 3)])
            self.relay.append([half(cols, left, LOW, at.along_x(1)), half(cols, right, HIGH, at.along_x(3))])

    def first(self):
        start(self.perm, *self.b, self.own)

    def second(self):
        arrive(self.perm)
        start(self.zl, *self.near[0])

    def third(self):
        arrive(self.zl, *self.b, *self.near[0])
        start(*self.near[1], *self.relay[0], *self.bfar, *self.fwd)

    def fourth(self):
        arrive(*self.near[1], *self.bfar)
        start(*self.relay[1], self.fwdfar)

    def last(self):
        arrive(self.own, *self.relay[0], *self.relay[1], *self.fwd, self.fwdfar)


class Scatter16:
    def __init__(self, at, piece, buf, send, recv):
        self.at, self.piece, self.buf, self.send, self.recv = at, piece, buf, send, recv
        self.source = (at.r == 0) & (at.c < 4)
        self.target = at.d > 0
        slot = buf.at[at.r, at.zh, at.core]
        self.incoming = pltpu.make_async_remote_copy(
            src_ref=slot, dst_ref=slot, send_sem=send.at[0], recv_sem=recv.at[0], device_id=at.partner, device_id_type=MESH
        )

    def device(self, i):
        return {"row": 2 * self.at.c + i // 8, "col": i % 8}

    def each(self, f):
        def step(i, _):
            pl.when((self.at.c > 0) | (i > 0))(lambda: f(i))
            return 0

        @pl.when(self.source)
        def _():
            lax.fori_loop(0, 16, step, 0)

    def copy(self, i):
        to = self.device(i)
        return pltpu.make_async_remote_copy(
            src_ref=self.piece(i), dst_ref=self.buf.at[to["row"], to["col"] // 2, to["col"] % 2],
            send_sem=self.send.at[i], recv_sem=self.recv.at[0], device_id=to, device_id_type=MESH,
        )

    def greet(self, greet):
        self.each(lambda i: greet(self.device(i)))
        pl.when(self.target)(lambda: greet({"row": 0, "col": self.at.x}))
        n = jnp.where(self.source, 16 - (self.at.c == 0).astype(jnp.int32), 0)
        return n + self.target.astype(jnp.int32)

    def first(self):
        self.each(lambda i: self.copy(i).start())

    def arrive(self):
        pl.when(self.target)(self.incoming.wait_recv)

    def drain(self):
        self.each(lambda i: self.copy(i).wait_send())


def inputs_kernel(fr, m, m16, anc, inv, mr, mc, g0, own_a, g, send, recv, s16, r16, sa, ra, la, *scr):
    at = Place()
    copies = Copies(send, recv)
    fronts = Spread64(at, copies, g, fr)
    lead = Spread64(at, copies, g0, g0.at[at.r, at.zh, at.core])
    blocks = Blocks(at, copies, mr, mc, m)
    scatter = Scatter16(at, lambda i: m16.at[i], g0, s16, r16)
    here = at.zh == at.l
    left = at.c == 0
    corner = left & (at.l == 0)

    def handed(e):
        rows = pl.ds(pl.multiple_of(256 * at.l + 128 * e, 128), 128)
        return pltpu.make_async_remote_copy(
            src_ref=anc.at[rows, pl.ds(0, 512)], dst_ref=own_a, send_sem=sa.at[e], recv_sem=ra.at[0],
            device_id={"col": 2 * at.l + e}, device_id_type=MESH,
        )

    hand = [(handed(0), left & (at.l > 0)), (handed(1), left)]
    kept = pltpu.make_async_copy(anc.at[pl.ds(0, 128), pl.ds(0, 512)], own_a, la)
    over_y = [
        (pltpu.make_async_remote_copy(
            src_ref=own_a, dst_ref=own_a, send_sem=sa.at[1 + k], recv_sem=ra.at[1],
            device_id=at.along_y(k), device_id_type=MESH,
        ), here)
        for k in range(1, 4)
    ]
    cross = at.core == 1
    extra = [
        (left & (at.l > 0), {"col": 2 * at.l + 1}),
        (here & cross & (at.l > 0), {"col": 0}),
    ]
    barrier, greet, total = meet(at, extra)
    total = total + scatter.greet(greet)
    pl.semaphore_wait(barrier, total)

    fronts.first()
    scatter.first()
    g[at.r, at.zh, at.core] = fr[...]
    mr[at.c] = m[...]

    @pl.when(at.r == at.c)
    def _():
        mc[at.r] = m[...]

    @pl.when(at.d == 0)
    def _():
        g0[0, 0, 0] = m16[0]

    fronts.second()
    blocks.first()
    start(*hand)
    pl.when(corner)(kept.start)
    fronts.third()
    fronts.last()

    def stage0():
        scatter.arrive()
        lead.first()
        blocks.second()

    def stage1():
        lead.second()
        blocks.third()
        pl.when(corner)(kept.wait)
        pl.when(here & jnp.logical_not(corner))(hand[0][0].wait_recv)
        start(*over_y)

    def stage2():
        lead.third()
        blocks.fourth()

    a, y, dt, xr = (scr[i * 2:(i + 1) * 2] for i in range(4))

    def move(r, _):
        for zh in range(4):
            for core in range(2):
                rows = pl.ds(pl.multiple_of(64 * r + 16 * zh + 8 * core, 8), 8)
                for p in range(2):
                    a[p][rows, :] = g[r, zh, core, p].astype(F32)
        return 0

    lax.fori_loop(0, 8, move, 0)
    chol_steps(a, y, dt, xr, [stage0, stage1, stage2])
    for p in range(2):
        inv[p] = y[p][...].astype(BF16)
    blocks.last()
    lead.last()
    pl.when(jnp.logical_not(here))(over_y[0][0].wait_recv)
    for copy, when in over_y + hand:
        pl.when(when)(copy.wait_send)
    copies.drain()
    scatter.drain()


def sems(n):
    return pltpu.SemaphoreType.DMA((n,))


def gather_inputs(fr, m, anc):
    s = jax.ShapeDtypeStruct
    vm = pl.BlockSpec(memory_space=VM)
    return pl.pallas_call(
        inputs_kernel,
        out_shape=[
            s((2, N, N), BF16), s((8, 128, 1024), BF16), s((8, 128, 1024), BF16), s((8, 4, 2, 8, 1024), BF16), s((128, 512), F32),
        ],
        in_specs=[vm, vm, vm, pl.BlockSpec(memory_space=pl.ANY)],
        out_specs=[vm] * 5,
        scratch_shapes=[
            pltpu.VMEM((8, 4, 2, 2, 8, 512), BF16), sems(48), sems(48), sems(16), sems(1), sems(5), sems(2),
            pltpu.SemaphoreType.DMA, *chol_scratch(2),
        ],
        compiler_params=pltpu.CompilerParams(has_side_effects=True, collective_id=1),
    )(fr, m, m.reshape(16, 8, 1024), anc)


def pivot_kernel(q, own_a, pinv, lead, cr, cc, gp, parts, send, recv, s16, r16, a, dt, xr):
    at = Place()
    copies = Copies(send, recv)
    ys = [copies.new(q, parts.at[at.l], at.along_y(k)) for k in range(1, 4)]
    spread = Spread64(at, copies, gp, gp.at[at.r, at.zh, at.core])
    blocks = Blocks(at, copies, cr, cc, lead)
    scatter = Scatter16(at, lambda i: lead.at[pl.ds(pl.multiple_of(8 * i, 8), 8)], gp, s16, r16)
    barrier, greet, total = meet(at)
    total = total + scatter.greet(greet)
    pl.semaphore_wait(barrier, total)
    start(*ys)
    parts[at.l] = q[...]
    arrive(*ys)
    terms = [parts[i].astype(F32) for i in range(4)]
    lead[...] = own_a[...] - (((terms[0] + terms[1]) + terms[2]) + terms[3])
    scatter.first()
    cr[at.c] = lead[...]

    @pl.when(at.r == at.c)
    def _():
        cc[at.r] = lead[...]

    @pl.when(at.d == 0)
    def _():
        gp[0, 0, 0] = lead[0:8, :]

    scatter.arrive()
    spread.first()
    spread.second()
    blocks.first()
    spread.third()
    spread.last()

    def move(r, _):
        for zh in range(4):
            for core in range(2):
                a[pl.ds(pl.multiple_of(64 * r + 16 * zh + 8 * core, 8), 8), :] = gp[r, zh, core]
        return 0

    lax.fori_loop(0, 8, move, 0)
    chol_steps([a], [pinv], [dt], [xr], [blocks.second, blocks.third, blocks.fourth])
    blocks.last()
    copies.drain()
    scatter.drain()


def gather_pivot(q, own_a):
    s = jax.ShapeDtypeStruct
    vm = pl.BlockSpec(memory_space=VM)
    return pl.pallas_call(
        pivot_kernel,
        out_shape=[s((N, N), F32), s((128, 512), F32), s((8, 128, 512), F32), s((8, 128, 512), F32)],
        in_specs=[vm, vm],
        out_specs=[vm] * 4,
        scratch_shapes=[
            pltpu.VMEM((8, 4, 2, 8, 512), F32), pltpu.VMEM((4, 128, 512), BF16), sems(40), sems(40), sems(16), sems(1),
            *chol_scratch(1, False),
        ],
        compiler_params=pltpu.CompilerParams(has_side_effects=True, collective_id=2),
        cost_estimate=pl.CostEstimate(flops=4_000_000_000, bytes_accessed=8_000_000, transcendentals=0),
    )(q, own_a)


def local(ancestor, coupling, fronts, tile_pattern):
    r, c = lax.axis_index("row"), lax.axis_index("col")
    fr = jnp.swapaxes(fronts[0], 1, 2).astype(BF16)
    on = lax.dynamic_slice_in_dim(tile_pattern[0], r, 1, 1)
    masked = coupling[0] * jnp.repeat(on[:, 0], 512)[None, :].astype(BF16)
    inv, mr, mc, m0, own_a = gather_inputs(fr, masked, ancestor)

    def solved(rows):
        out = [
            lax.dot_general(rows[:, p * 512:(p + 1) * 512], inv[p], (((1,), (1,)), ((), ())), preferred_element_type=F32)
            for p in range(2)
        ]
        return jnp.concatenate(out, 1).astype(BF16)

    outer = lambda a, b: lax.dot_general(a, b, (((1,), (1,)), ((), ())), preferred_element_type=F32)
    q = outer(solved(masked), solved(m0.reshape(512, 1024))).astype(BF16)
    row_side, col_side = solved(mr.reshape(1024, 1024)), solved(mc.reshape(1024, 1024))
    update = outer(row_side, col_side).astype(BF16)
    q, update = lax.optimization_barrier((q, update))
    summed = lax.psum(update, "layer")
    pinv, lead, cr, cc = gather_pivot(q, own_a)
    high = functools.partial(
        lax.dot_general, dimension_numbers=(((1,), (1,)), ((), ())), precision=lax.Precision.HIGH, preferred_element_type=F32
    )
    rows = high(cr.reshape(1024, 512), pinv)
    cols = high(cc.reshape(1024, 512), pinv)
    schur = ancestor - summed.astype(F32) - high(rows, cols)
    panel = high(lead, pinv)
    scale = jnp.diagonal(lax.dynamic_slice(pinv, (8 * (8 * r + c), 0), (8, 512)).reshape(8, 64, 8)[:, 8 * r + c])
    return schur, panel, 1.0 / (scale * scale)


def solution(mesh):
    return jax.shard_map(
        local,
        mesh=mesh,
        in_specs=(
            P("row", "col"),
            P("layer", ("row", "col"), None),
            P("layer", None, None, ("row", "col")),
            P("layer", None, None),
        ),
        out_specs=(P("row", "col"), P(("row", "col"), None), P(("row", "col"))),
        check_vma=False,
    )
```

time: 318 us -> 209 us (0.66)
  Pallas kernels: 229 us -> 156 us
  waiting for transfers between devices: 36.7 us -> 0.02 us
    pallas_call x4 -> x2, Pallas kernels: 229 us -> 156 us  [the longest x1 84.7 us: gather_pivot(): pl.pallas_call(pivot_kernel, out_shape=[s((N, N), F32), s((128, 512), F32...]
    reduce_scatter x1 -> x0, waiting for transfers between devices: 36.7 us -> none  [local(): share = lax.psum_scatter(update, 'layer', scatter_dimension=0, tiled=True)]
  transfers between devices with their start and end apart: 2 -> 1, of which waited for: 1 -> 0; matrix products, arithmetic and copies ran while one was open for 4% -> 6% of each run, Pallas kernels for 38% -> 41%
where the time goes in v2:
time: 209 us; the launch traced here: 208 us
  Pallas kernels  156 us (75%)
  matrix products  27.8 us (13%)
  between operations  14.2 us (7%)
  other arithmetic  6.11 us (3%)
  local copies, waits for them, and re-layouts  3.06 us (1%)
    pallas_call x1, Pallas kernels, gather_pivot(): pl.pallas_call(pivot_kernel, out_shape=[s((N, N), F32), s((128, 512), F32...  84.7 us
    pallas_call x1, Pallas kernels, gather_inputs(): pl.pallas_call(inputs_kernel, out_shape=[s((2, N, N), BF16), s((8, 128, 1...  71.7 us
    dot_general x1, matrix products, local(): schur = ancestor - summed.astype(F32) - high(rows, cols)  7.59 us
    dot_general x8, matrix products, solved(): lax.dot_general(rows[:, p * 512:(p + 1) * 512], inv[p], (((1,), (1,)), ((...  6.02 us
    dot_general x2, matrix products, local(): lax.dot_general(a, b, (((1,), (1,)), ((), ())), preferred_element_type=F32)  4.81 us
  transfers between devices with their start and end apart: 1, of which 0 were waited for; matrix products, arithmetic and copies ran while one was open for 6% of the time, Pallas kernels for 41%

profile of v2, /device:TPU:1, one launch (start us, length us, event | category | flops | bytes accessed | tf_op | source)
XLA Modules:
  0.0 207.7 jit_solution(8795088106098373728)
XLA Ops:
  7.2 0.0 all-reduce.2.cloned.1.call-start
  7.2 0.9 fusion.42
  8.1 0.1 broadcast_bitcast_fusion
  8.2 1.7 bitcast_multiply_fusion.1.m
  9.8 1.7 bitcast_multiply_fusion.m16
  11.5 1.4 convert_bitcast_fusion.fr
  12.9 71.7 %shard_map.67 = (bf16[2,512,512]{2,1,0:T(8,128)(2,1)}, bf16[8,128,1024]{2,1,0:T(8,128)(2,1)}, bf16[8,128,1024]{2,1,0:T(8,128)(2,1)}, bf16[8,4,2,8,1024]{4,3,2,1,0:T(8,128)(2,1)}, f32[128,512]{1,0:T(8,128)}) custom-call(bf16[2,8,512]{2,1,0:T(8,128)(2,1)} %convert_bitcast_fusion.fr, bf16[128,1024]{1,0:T(8,128)(2,1)} %bitcast_multiply_fusion.1.m, ...), custom_call_target="tpu_custom_call" | custom-call | tf_op jit(solution)/shard_map/pallas_call | solution.py:390
  84.6 0.0 copy-start.4
  84.6 0.0 copy-start.5
  84.6 2.2 %convolution_convert_fusion.3 = bf16[1024,512]{1,0:T(8,128)(2,1)S(1)} fusion(bf16[1024,1024]{1,0:T(8,128)(2,1)} %bitcast.52, bf16[2,512,512]{2,1,0:T(8,128)(2,1)} %get-tuple-element.14), kind=kOutput, calls=%fused_computation.13 | convolution fusion | flops 537395200 | bytes 2621440 | tf_op jit(solution)/shard_map/dot_general | solution.py:477
  86.9 0.0 copy-done.4
  86.9 0.0 copy-done.5
  86.9 0.0 copy-start.3
  86.9 0.7 convolution_convert_fusion.2
  87.7 0.8 copy-done.3
  88.5 0.7 convolution_convert_fusion.1
  89.2 0.0 copy-start.6
  89.3 0.7 convolution_convert_fusion
  90.0 0.0 copy-start.2
  90.0 0.5 copy-done.6
  90.5 0.5 convolution_convert_fusion.5
  91.0 0.5 convolution_convert_fusion.4
  91.4 0.0 copy-done.2
  91.4 0.3 convolution_convert_fusion.6
  91.8 0.3 convolution_convert_fusion.7
  92.1 3.7 %fusion.7 = bf16[1024,1024]{1,0:T(8,128)(2,1)} fusion(bf16[1024,512]{1,0:T(8,128)(2,1)S(1)} %convolution_convert_fusion, bf16[1024,512]{1,0:T(8,128)(2,1)S(1)} %convolution_convert_fusion.1, bf16[1024,512]{1,0:T(8,128)(2,1)S(1)} %convolution_convert_fusion.2, bf16[1024,512]{1,0:T(8,128)(2,1)S(1)} %convolution_convert_fusion.3), kind=kOutput, calls=%fused_computation.9 | convolution fusion | flops 2156920832 | bytes 6291456 | tf_op jit(solution)/shard_map/dot_general | solution.py:482
  95.8 1.1 convolution_convert_fusion.8.q
  96.9 0.0 all-reduce.2.cloned.1.call-update
  96.9 84.7 %shard_map.68 = (f32[512,512]{1,0:T(8,128)}, f32[128,512]{1,0:T(8,128)}, f32[8,128,512]{2,1,0:T(8,128)}, f32[8,128,512]{2,1,0:T(8,128)}) custom-call(bf16[128,512]{1,0:T(8,128)(2,1)} %convolution_convert_fusion.8.q, f32[128,512]{1,0:T(8,128)} %get-tuple-element.20.own_a), custom_call_target="tpu_custom_call" | custom-call | flops 4000000000 | bytes 8000000 | tf_op jit(solution)/shard_map/pallas_call | solution.py:454
  181.7 0.0 copy-start
  181.7 0.8 constant_dynamic-slice_fusion.1
  182.5 0.2 reshape.48
  182.7 0.6 gather_fusion
  183.3 0.5 multiply_divide_fusion
  183.8 2.7 %fusion.47 = f32[128,512]{1,0:T(8,128)} fusion(f32[128,512]{1,0:T(8,128)} %get-tuple-element.24, f32[512,512]{1,0:T(8,128)} %get-tuple-element.22), kind=kOutput, calls=%fused_computation.63 | convolution fusion | flops 201326592 | bytes 1572864 | tf_op jit(solution)/shard_map/dot_general | solution.py:495
  186.5 0.0 copy-done
  186.5 0.0 copy-start.1
  186.5 3.6 %fusion.46 = f32[1024,512]{1,0:T(8,128)S(1)} fusion(f32[1024,512]{1,0:T(8,128)} %bitcast.47, f32[512,512]{1,0:T(8,128)S(1)} %copy-done), kind=kOutput, calls=%fused_computation.62 | convolution fusion | flops 1610612736 | bytes 5242880 | tf_op jit(solution)/shard_map/dot_general | solution.py:493
  190.1 0.0 copy-done.1
  190.1 3.2 %fusion.45 = f32[1024,512]{1,0:T(8,128)} fusion(f32[1024,512]{1,0:T(8,128)S(1)} %bitcast.46, f32[512,512]{1,0:T(8,128)S(1)} %copy-done), kind=kOutput, calls=%fused_computation.61 | convolution fusion | flops 1610612736 | bytes 5242880 | tf_op jit(solution)/shard_map/dot_general | solution.py:492
  193.3 0.0 all-reduce.2.cloned.1.call-done
  193.3 7.6 %subtract_subtract_fusion = f32[1024,1024]{1,0:T(8,128)} fusion(f32[1024,1024]{1,0:T(8,128)} %anc.1, bf16[1024,1024]{1,0:T(8,128)(2,1)} %all-reduce.2.cloned.1.call-done, f32[1024,512]{1,0:T(8,128)} %fusion.45, f32[1024,512]{1,0:T(8,128)S(1)} %fusion.46), kind=kOutput, calls=%fused_computation.1 | convolution fusion | flops 3224371200 | bytes 14680064 | tf_op jit(solution)/shard_map/dot_general | solution.py:494
  (3 shorter events, 0.0 us)
Async XLA Ops:
  7.2 186.1 %all-reduce.2.cloned.1.call-start = ((), (), s32[]{:S(2)}) async-start(), calls=%async_computation | async-start | bytes 4194304 | tf_op jit(solution)/shard_map/psum | solution.py:487
  84.6 2.3 %copy-start.4 = (bf16[8,128,1024]{2,1,0:T(8,128)(2,1)S(1)}, bf16[8,128,1024]{2,1,0:T(8,128)(2,1)}, u32[]{:S(2)}) copy-start(bf16[8,128,1024]{2,1,0:T(8,128)(2,1)} %get-tuple-element.16) | copy-start | bytes 6291460
  84.6 2.3 %copy-start.5 = (bf16[2,512,512]{2,1,0:T(8,128)(2,1)S(1)}, bf16[2,512,512]{2,1,0:T(8,128)(2,1)}, u32[]{:S(2)}) copy-start(bf16[2,512,512]{2,1,0:T(8,128)(2,1)} %get-tuple-element.14) | copy-start | bytes 3145732
  86.9 1.6 copy-start.3
  89.2 1.2 copy-start.6
  90.0 1.4 copy-start.2
  181.7 4.9 %copy-start = (f32[512,512]{1,0:T(8,128)S(1)}, f32[512,512]{1,0:T(8,128)}, u32[]{:S(2)}) copy-start(f32[512,512]{1,0:T(8,128)} %get-tuple-element.22) | copy-start | bytes 3145732
  186.5 3.6 %copy-start.1 = (f32[8,128,512]{2,1,0:T(8,128)S(1)}, f32[8,128,512]{2,1,0:T(8,128)}, u32[]{:S(2)}) copy-start(f32[8,128,512]{2,1,0:T(8,128)} %get-tuple-element.21) | copy-start | bytes 6291460
Sparse Core Ops, SparseCore 0:
  97.0 71.0 all-reduce.1
